TPU v7x, 32 devices: a whole 2x2x4 slice. The times are simulated.
32 devices in a mesh: groups: 2 (over y), head: 4 (over z), state: 4 (over x, core).
Axes of the slice: x: 2, y: 2, z: 4, core: 2. Of those that a mesh axis runs over, the one named last changes fastest.
Arguments:
- tokens: bfloat16 [32, 2048], P(('groups', 'head'), 'state'), parts along dimension 0, may hold values from -20 to 20
- mixer_norm: float32 [2048], P('state'), may hold values from 0.1 to 1.9
- input_proj: bfloat16 [2, 2048, 8192], P(None, 'state', 'head'), may hold values from -0.125 to 0.125
- conv_weight: float32 [4, 8192], P(None, 'head'), may hold values from -3 to 3
- conv_bias: float32 [8192], P('head'), may hold values from -3 to 3
- conv_state: float32 [3, 32, 8192], P(None, 'groups', 'head'), parts along dimension 1, may hold values from -6 to 6
- state_proj: bfloat16 [8192, 288], P('head'), may hold values from -0.125 to 0.125
- step_gain: float32 [256], replicated, may hold values from 0.1 to 1.9
- step_proj: bfloat16 [256, 8192], P(None, 'head'), may hold values from -0.375 to 0.375
- step_bias: float32 [8192], P('head'), may hold values from -6 to -1
- decay_log: float32 [16, 8192], P('state', 'head'), may hold values from 0 to 2.77
- skip_gain: float32 [8192], P('head'), may hold values from 0.5 to 1.5
- ssm_state: float32 [16, 32, 8192], P('state', 'groups', 'head'), parts along dimension 1, may hold values from -6 to 6
- output_proj: bfloat16 [8192, 2048], P('head', 'state'), may hold values from -0.0625 to 0.0625
- moe_norm: float32 [2048], replicated, may hold values from 0.1 to 1.9
- router_weight: float32 [2048, 8], replicated, may hold values from -0.125 to 0.125
- expert_ids: int32 [32, 2], P(('groups', 'head')), parts along dimension 0, may hold values from 0 to 7, as said below
- slot_ids: int32 [32, 2], P(('groups', 'head')), parts along dimension 0, may hold values from 0 to 3, as said below
- gate_proj: bfloat16 [8, 2048, 7168], P('head', None, 'state'), may hold values from -0.125 to 0.125
- up_proj: bfloat16 [8, 2048, 7168], P('head', None, 'state'), may hold values from -0.125 to 0.125
- down_proj: bfloat16 [8, 7168, 2048], P('head', 'state'), may hold values from -0.0625 to 0.0625
Outputs:
- layer_out: bfloat16 [32, 2048], P(('groups', 'head'), 'state'), parts along dimension 0
- new_conv: float32 [3, 32, 8192], P(None, 'groups', 'head'), parts along dimension 1
- new_state: float32 [16, 32, 8192], P('state', 'groups', 'head'), parts along dimension 1
- expert_load: float32 [16], P('groups'), parts along dimension 0
- aux_loss: float32 [2], P('groups'), parts along dimension 0
There are 2 independent parts, one for each index of `groups`. A program takes and returns all parts, laid end to end along the dimension named above; an argument that names none is the same for every part. Nothing has to cross between parts.
Inputs may be any that keep to these rules, and one draw needn't show every extreme that they name: `expert_ids`: each row names 2 different experts. One expert, the same on every device, is named by every row. `slot_ids`: among the choices of one aligned block of 4 rows that name one expert, the slot positions are distinct and run from 0 to their count less one.
All inputs are finite; a program needn't handle non-finite values.
Results may differ from a plain program's by a relative error of at most 0.007.
Values may be sent and summed in bfloat16 or wider, within the bound.
A program may use at most 128 MiB of HBM per device.

v0:
```python
import jax
import jax.numpy as jnp
from jax import lax
from jax.sharding import PartitionSpec as P

D = 2048
D_STATE = 16
DT_RANK = 256
EXPERTS = 8
TOPK = 2
CAP = 2
NORM_EPS = 1e-05
STEP_EPS = 1e-06


def expert_ffn(received, gate_proj, up_proj, down_proj):
    gate_val = jnp.einsum("nlcd,ldf->nlcf", received, gate_proj, preferred_element_type=jnp.float32)
    up_val = jnp.einsum("nlcd,ldf->nlcf", received, up_proj, preferred_element_type=jnp.float32)
    hidden = (jax.nn.silu(gate_val) * up_val).astype(jnp.bfloat16)
    return jnp.einsum("nlcf,lfd->nlcd", hidden, down_proj, preferred_element_type=jnp.float32)


def per_device(
    tokens,
    mixer_norm,
    input_proj,
    conv_weight,
    conv_bias,
    conv_state,
    state_proj,
    step_gain,
    step_proj,
    step_bias,
    decay_log,
    skip_gain,
    ssm_state,
    output_proj,
    moe_norm,
    router_weight,
    expert_ids,
    slot_ids,
    gate_proj,
    up_proj,
    down_proj,
):
    head_count = lax.axis_size("head")
    state_index = lax.axis_index("state")
    own_rows = tokens.shape[0]
    tok_f32 = tokens.astype(jnp.float32)
    first_sq = lax.psum(jnp.sum(tok_f32 * tok_f32, axis=1), "state")
    inv_first = lax.rsqrt(first_sq / D + NORM_EPS)[:, None]
    normed = (tok_f32 * inv_first * mixer_norm).astype(jnp.bfloat16)
    branch_part = jnp.einsum(
        "td,kdc->ktc",
        lax.all_gather(normed, "head", axis=0, tiled=True),
        input_proj,
        preferred_element_type=jnp.float32,
    )
    branch_full = lax.psum(branch_part, "state")
    conv_input = branch_full[0]
    gate_branch = branch_full[1]
    window = jnp.concatenate([conv_state, conv_input[None]], axis=0)
    conv_out = jax.nn.silu(jnp.sum(conv_weight[:, None, :] * window, axis=0) + conv_bias)
    new_conv = window[1:]
    proj_part = jnp.dot(
        conv_out.astype(jnp.bfloat16), state_proj, preferred_element_type=jnp.float32
    )
    projected = lax.psum(proj_part, "head")
    step_low = projected[:, :DT_RANK]
    state_slab = decay_log.shape[0]
    b_input = lax.dynamic_slice_in_dim(projected, DT_RANK + state_index * state_slab, state_slab, 1)
    c_output = lax.dynamic_slice_in_dim(
        projected, DT_RANK + D_STATE + state_index * state_slab, state_slab, 1
    )
    step_inv = lax.rsqrt(jnp.mean(step_low * step_low, axis=1, keepdims=True) + STEP_EPS)
    step_normed = (step_low * step_inv * step_gain).astype(jnp.bfloat16)
    step_size = jax.nn.softplus(
        jnp.dot(step_normed, step_proj, preferred_element_type=jnp.float32) + step_bias
    )
    decay_rate = jnp.exp(-step_size[None] * jnp.exp(decay_log)[:, None, :])
    new_state = decay_rate * ssm_state + step_size[None] * b_input.T[:, :, None] * conv_out[None]
    read_part = jnp.sum(c_output.T[:, :, None] * new_state, axis=0)
    readout = lax.psum(read_part, "state")
    mixer_act = ((readout + skip_gain * conv_out) * jax.nn.silu(gate_branch)).astype(jnp.bfloat16)
    mixer_sum = lax.psum_scatter(
        jnp.dot(mixer_act, output_proj, preferred_element_type=jnp.float32),
        "head",
        scatter_dimension=0,
        tiled=True,
    )
    residual = (tok_f32 + mixer_sum).astype(jnp.bfloat16)
    full_rows = lax.all_gather(residual, "state", axis=1, tiled=True).astype(jnp.float32)
    inv_second = lax.rsqrt(jnp.mean(full_rows * full_rows, axis=1, keepdims=True) + NORM_EPS)
    scaled = full_rows * moe_norm
    logits = inv_second * jnp.dot(scaled, router_weight, precision=lax.Precision.HIGHEST)
    row_normed = (scaled * inv_second).astype(jnp.bfloat16)
    expert_hit = expert_ids[:, :, None] == jnp.arange(EXPERTS, dtype=jnp.int32)[None, None, :]
    chosen = jnp.sum(jnp.where(expert_hit, logits[:, None, :], 0.0), axis=2)
    gate_probs = jax.nn.sigmoid(chosen - chosen[:, ::-1])
    kept_mask = slot_ids < CAP
    mix_weight = jnp.where(kept_mask, gate_probs, 0.0)
    slot_hit = slot_ids[:, :, None] == jnp.arange(CAP, dtype=jnp.int32)[None, None, :]
    slot_place = expert_hit[:, :, :, None] & slot_hit[:, :, None, :]
    dispatch = jnp.sum(slot_place.astype(jnp.int32), axis=1).astype(jnp.bfloat16)
    combine_weight = jnp.sum(jnp.where(slot_place, mix_weight[:, :, None, None], 0.0), axis=1)
    outgoing = jnp.einsum(
        "tec,td->ecd", dispatch, row_normed, preferred_element_type=jnp.float32
    ).astype(jnp.bfloat16)
    row_width = outgoing.shape[2]
    local_experts = gate_proj.shape[0]
    expert_groups = EXPERTS // local_experts
    copies = head_count * local_experts // EXPERTS
    outgoing = jnp.broadcast_to(
        outgoing.reshape(expert_groups, 1, local_experts, CAP, row_width),
        (expert_groups, copies, local_experts, CAP, row_width),
    )
    outgoing = outgoing.reshape(head_count, local_experts, CAP, row_width)
    partial_out = expert_ffn(
        lax.all_to_all(outgoing, "head", split_axis=0, concat_axis=0, tiled=True),
        gate_proj,
        up_proj,
        down_proj,
    )
    returned = lax.all_to_all(
        partial_out.astype(jnp.bfloat16), "head", split_axis=0, concat_axis=0, tiled=True
    ).astype(partial_out.dtype)
    per_expert = returned.reshape(expert_groups, copies, local_experts, CAP, row_width).sum(axis=1)
    per_expert = per_expert.reshape(EXPERTS, CAP, row_width)
    expert_mix = jnp.einsum(
        "tec,ecd->td", combine_weight, per_expert, precision=lax.Precision.HIGHEST
    )
    expert_mix = lax.psum_scatter(
        expert_mix.astype(jnp.bfloat16), "state", scatter_dimension=1, tiled=True
    ).astype(jnp.float32)
    layer_out = (residual.astype(jnp.float32) + expert_mix).astype(jnp.bfloat16)
    load_own = jnp.sum(jnp.where(expert_hit & kept_mask[:, :, None], 1.0, 0.0), axis=(0, 1)).astype(
        jnp.float32
    )
    prob_own = jnp.sum(jax.nn.sigmoid(logits), axis=0)
    load_sum, prob_sum = lax.psum((load_own, prob_own), "head")
    total_rows = head_count * own_rows
    aux_value = EXPERTS * jnp.sum(load_sum / (total_rows * TOPK) * (prob_sum / total_rows))
    return (layer_out, new_conv, new_state, load_sum, aux_value.reshape(1))


def solution(mesh):
    return jax.shard_map(
        per_device,
        mesh=mesh,
        in_specs=(
            P(("groups", "head"), "state"),
            P("state"),
            P(None, "state", "head"),
            P(None, "head"),
            P("head"),
            P(None, "groups", "head"),
            P("head", None),
            P(),
            P(None, "head"),
            P("head"),
            P("state", "head"),
            P("head"),
            P("state", "groups", "head"),
            P("head", "state"),
            P(),
            P(),
            P(("groups", "head"), None),
            P(("groups", "head"), None),
            P("head", None, "state"),
            P("head", None, "state"),
            P("head", "state", None),
        ),
        out_specs=(
            P(("groups", "head"), "state"),
            P(None, "groups", "head"),
            P("state", "groups", "head"),
            P("groups"),
            P("groups"),
        ),
        check_vma=False,
    )
```

profile of v0, /device:TPU:0, one launch (start us, length us, event | category | flops | bytes accessed | tf_op | source)
XLA Modules:
  0.0 225.7 jit_solution(13633011839943154887)
XLA Ops:
  7.2 0.9 fusion.46
  8.2 8.4 %psum.42 = f32[4]{0:T(128)S(1)} all-reduce(f32[4]{0:T(128)S(1)} %fusion.46), channel_id=1, replica_groups=mesh['groups'=2,'head'=4,'state'=4] {'state'}, use_global_device_ids=true, to_apply=%region_1.0 | all-reduce | flops 4 | bytes 32 | tf_op jit(solution)/shard_map/psum | solution.py:50
  16.6 0.8 fusion.52
  17.4 13.4 %all-gather = bf16[4,4,512]{2,1,0:T(4,128)(2,1)S(1)} all-gather(bf16[1,4,512]{2,1,0:T(4,128)(2,1)S(1)} %fusion.52), channel_id=1, replica_groups=mesh['groups'=2,'head'=4,'state'=4] {'head'}, dimensions={0}, use_global_device_ids=true | all-gather | bytes 20480 | tf_op jit(solution)/shard_map/all_gather | solution.py:55
  30.8 3.6 %convolution_bitcast_fusion = f32[2,16,2048]{2,1,0:T(8,128)} fusion(bf16[16,512,1]{1,0,2:T(8,128)(2,1)S(1)} %reshape.86, bf16[2,512,2048]{2,1,0:T(8,128)(2,1)} %param.23), kind=kOutput, calls=%fused_computation.6 | convolution fusion | flops 67108864 | bytes 4472832 | tf_op jit(solution)/shard_map/td,kdc->ktc/dot_general | solution.py:53
  34.4 0.8 iota_compare_fusion
  36.5 0.8 exp.33
  37.3 1.2 dynamic-slice
  39.3 27.6 %all-reduce.5.cloned.1.call-done = f32[2,16,2048]{2,1,0:T(8,128)} async-done(((f32[2,16,2048]{2,1,0:T(8,128)}), f32[2,16,2048]{2,1,0:T(8,128)}) %all-reduce.5.cloned.1.call-update) | async-done | bytes 262160 | tf_op jit(solution)/shard_map/psum | solution.py:59
  66.9 0.9 slice.16
  67.8 1.1 fusion.26
  69.6 1.7 fusion.31
  71.3 19.0 %psum.44 = f32[16,288]{1,0:T(8,128)S(1)} all-reduce(f32[16,288]{1,0:T(8,128)S(1)} %fusion.31), channel_id=1, replica_groups=mesh['groups'=2,'head'=4,'state'=4] {'head'}, use_global_device_ids=true, to_apply=%region_4.5 | all-reduce | flops 4608 | bytes 36864 | tf_op jit(solution)/shard_map/psum | solution.py:68
  90.7 1.5 fusion.56
  92.2 2.7 %multiply_reduce_fusion = (f32[16,2048]{1,0:T(8,128)}, f32[4,16,2048]{2,1,0:T(8,128)}) fusion(f32[4,16]{1,0:T(4,128)S(1)} %copy.53, f32[16,2048]{1,0:T(8,128)S(1)} %divide_multiply_fusion, f32[4,16]{1,0:T(4,128)S(1)} %copy.54, f32[16,2048]{1,0:T(8,128)S(1)} %get-tuple-element.14, f32[4,16,2048]{2,1,0:T(8,128)} %param.33, f32[4,2048]{1,0:T(4,128)S(1)} %exp.33, ...), kind=kLoop, calls=%fused_computation.23 | loop fusion | flops 884736 | bytes 1606144 | tf_op jit(solution)/shard_map/reduce_sum | solution.py:82
  94.9 1.7 fusion.27
  96.6 27.5 %all-reduce.7.cloned.1.call-done = f32[16,2048]{1,0:T(8,128)} async-done(((f32[16,2048]{1,0:T(8,128)}), f32[16,2048]{1,0:T(8,128)}) %all-reduce.7.cloned.1.call-update) | async-done | bytes 131088 | tf_op jit(solution)/shard_map/psum | solution.py:83
  124.1 1.3 fusion.28
  125.5 19.0 %all-reduce = f32[16,512]{1,0:T(8,128)S(1)} all-reduce(f32[16,512]{1,0:T(8,128)S(1)} %fusion.28), channel_id=2, replica_groups=mesh['groups'=2,'head'=4,'state'=4] {'head'}, use_global_device_ids=true, to_apply=%region_8.9.clone | all-reduce | flops 8192 | bytes 65536
  145.2 5.2 %all_gather.7 = bf16[4,2048]{1,0:T(4,128)(2,1)S(1)} all-gather(bf16[4,512]{1,0:T(4,128)(2,1)S(1)} %fusion.49), channel_id=1, replica_groups=mesh['groups'=2,'head'=4,'state'=4] {'state'}, dimensions={1}, use_global_device_ids=true | all-gather | bytes 20480 | tf_op jit(solution)/shard_map/all_gather | solution.py:92
  150.5 1.1 fusion.54
  151.6 0.9 convolution_convert_fusion
  153.2 3.3 %all-to-all-start = ((bf16[4,2,2,2048]{3,2,1,0:T(2,128)(2,1)}), bf16[4,2,2,2048]{3,2,1,0:T(2,128)(2,1)S(1)}, u32[]{:S(2)}, u32[]{:S(2)}) async-start(bf16[4,2,2,2048]{3,2,1,0:T(2,128)(2,1)} %bitcast.6), calls=%async_computation | async-start | bytes 131072 | tf_op jit(solution)/shard_map/all_to_all | solution.py:119
  156.7 12.1 %all-reduce.1 = (f32[8]{0:T(128)S(1)}, f32[8]{0:T(128)S(1)}) all-reduce(f32[8]{0:T(128)S(1)} %get-tuple-element.5, f32[8]{0:T(128)S(1)} %get-tuple-element.15), channel_id=1, replica_groups=mesh['groups'=2,'head'=4,'state'=4] {'head'}, use_global_device_ids=true, to_apply=%region_15.16 | all-reduce | flops 16 | bytes 128 | tf_op jit(solution)/shard_map/psum | solution.py:140
  168.9 7.5 %fusion.6 = f32[4,2,2,1792]{3,0,2,1:T(4,128)S(1)} fusion(bf16[2,2048,1792]{2,1,0:T(8,128)(2,1)} %param.39, bf16[4,2,2,2048]{3,2,1,0:T(2,128)(2,1)S(1)} %all-to-all-done), kind=kOutput, calls=%fused_computation.7 | convolution fusion | flops 117440512 | bytes 14860288 | tf_op jit(solution)/shard_map/nlcd,ldf->nlcf/dot_general | solution.py:17
  176.4 7.5 %fusion.15 = bf16[4,2,2,1792]{3,0,2,1:T(4,128)(2,1)S(1)} fusion(bf16[2,2048,1792]{2,1,0:T(8,128)(2,1)} %param.40, f32[4,2,2,1792]{3,0,2,1:T(4,128)S(1)} %fusion.6, bf16[4,2,2,2048]{3,2,1,0:T(2,128)(2,1)S(1)} %all-to-all-done), kind=kOutput, calls=%fused_computation.11 | convolution fusion | flops 117612544 | bytes 14917632 | tf_op jit(solution)/shard_map/nlcd,ldf->nlcf/dot_general | solution.py:18
  183.9 2.1 fusion.21
  186.7 3.3 %all-to-all-start.1 = ((bf16[4,2,2,2048]{3,2,1,0:T(2,128)(2,1)}), bf16[4,2,2,2048]{3,2,1,0:T(2,128)(2,1)S(1)}, u32[]{:S(2)}, u32[]{:S(2)}) async-start(bf16[4,2,2,2048]{3,2,1,0:T(2,128)(2,1)} %copy.58), calls=%async_computation.1 | async-start | bytes 131072 | tf_op jit(solution)/shard_map/all_to_all | solution.py:124
  190.1 5.6 %all-to-all-done.1 = bf16[4,2,2,2048]{3,2,1,0:T(2,128)(2,1)S(1)} async-done(((bf16[4,2,2,2048]{3,2,1,0:T(2,128)(2,1)}), bf16[4,2,2,2048]{3,2,1,0:T(2,128)(2,1)S(1)}, u32[]{:S(2)}, u32[]{:S(2)}) %all-to-all-start.1) | async-done | bytes 65568 | tf_op jit(solution)/shard_map/all_to_all | solution.py:124
  196.0 1.1 copy.64
  198.3 18.1 %reduce-scatter.4.cloned.1.call-done = bf16[512,4]{1,0:T(8,128)(2,1)} async-done(((bf16[2048,4]{1,0:T(8,128)(2,1)}), bf16[512,4]{1,0:T(8,128)(2,1)}) %reduce-scatter.4.cloned.1.call-update) | async-done | bytes 4112
  216.4 1.0 copy.65
  (47 shorter events, 6.8 us)
Async XLA Ops:
  7.2 117.0 %copy-start = (bf16[2048,512]{1,0:T(8,128)(2,1)S(1)}, bf16[2048,512]{1,0:T(8,128)(2,1)}, u32[]{:S(2)}) copy-start(bf16[2048,512]{1,0:T(8,128)(2,1)} %param.34) | copy-start | bytes 6291460
  7.2 149.4 %copy-start.1 = (s32[4,2]{0,1:T(2,128)S(1)}, s32[4,2]{0,1:T(2,128)}, u32[]{:S(2)}) copy-start(s32[4,2]{0,1:T(2,128)} %param.37) | copy-start | bytes 100
  7.2 149.5 %copy-start.2 = (s32[4,2]{0,1:T(2,128)S(1)}, s32[4,2]{0,1:T(2,128)}, u32[]{:S(2)}) copy-start(s32[4,2]{0,1:T(2,128)} %param.38) | copy-start | bytes 100
  7.2 59.7 %all-reduce.5.cloned.1.call-start = ((), (), s32[]{:S(2)}) async-start(), calls=%async_computation.3 | async-start | bytes 524288 | tf_op jit(solution)/shard_map/psum | solution.py:59
  34.4 89.8 %all-reduce.7.cloned.1.call-start = ((), (), s32[]{:S(2)}) async-start(), calls=%async_computation.4 | async-start | bytes 262144 | tf_op jit(solution)/shard_map/psum | solution.py:83
  153.2 15.7 %all-to-all-start = ((bf16[4,2,2,2048]{3,2,1,0:T(2,128)(2,1)}), bf16[4,2,2,2048]{3,2,1,0:T(2,128)(2,1)S(1)}, u32[]{:S(2)}, u32[]{:S(2)}) async-start(bf16[4,2,2,2048]{3,2,1,0:T(2,128)(2,1)} %bitcast.6), calls=%async_computation | async-start | bytes 131072 | tf_op jit(solution)/shard_map/all_to_all | solution.py:119
  168.9 28.1 %copy-start.3 = (f32[8]{0:T(128)}, f32[8]{0:T(128)S(1)}, u32[]{:S(2)}) copy-start(f32[8]{0:T(128)S(1)} %get-tuple-element.7) | copy-start | bytes 100
  168.9 15.0 %slice-start = ((s8[14680064]{0:T(1024)(128)(4,1)}), s8[4194304]{0:T(1024)(128)(4,1)S(1)}, s32[]{:S(2)}) async-start(s8[14680064]{0:T(1024)(128)(4,1)} %bitcast.71), calls=%async_computation.6 | async-start | bytes 8388608
  168.9 15.0 %slice-start.1 = ((s8[14680064]{0:T(1024)(128)(4,1)}), s8[4194304]{0:T(1024)(128)(4,1)S(1)}, s32[]{:S(2)}) async-start(s8[14680064]{0:T(1024)(128)(4,1)} %bitcast.71), calls=%async_computation.7 | async-start | bytes 8388608
  176.4 7.5 %slice-start.2 = ((s8[14680064]{0:T(1024)(128)(4,1)}), s8[4194304]{0:T(1024)(128)(4,1)S(1)}, s32[]{:S(2)}) async-start(s8[14680064]{0:T(1024)(128)(4,1)} %bitcast.71), calls=%async_computation.8 | async-start | bytes 8388608
  176.4 7.5 %slice-start.3 = ((s8[14680064]{0:T(1024)(128)(4,1)}), s8[2097152]{0:T(1024)(128)(4,1)S(1)}, s32[]{:S(2)}) async-start(s8[14680064]{0:T(1024)(128)(4,1)} %bitcast.71), calls=%async_computation.9 | async-start | bytes 4194304
  186.7 9.0 %all-to-all-start.1 = ((bf16[4,2,2,2048]{3,2,1,0:T(2,128)(2,1)}), bf16[4,2,2,2048]{3,2,1,0:T(2,128)(2,1)S(1)}, u32[]{:S(2)}, u32[]{:S(2)}) async-start(bf16[4,2,2,2048]{3,2,1,0:T(2,128)(2,1)} %copy.58), calls=%async_computation.1 | async-start | bytes 131072 | tf_op jit(solution)/shard_map/all_to_all | solution.py:124
  190.0 26.4 %reduce-scatter.4.cloned.1.call-start = ((), (), s32[]{:S(2)}) async-start(), calls=%async_computation.5 | async-start | bytes 655360
Sparse Core Ops, SparseCore 0:
  34.5 32.3 all-reduce.4
  95.0 29.0 all-reduce.6
  197.2 19.2 reduce-scatter.3
where the time goes:
time: 227 us; the launch traced here: 226 us
  waiting for transfers between devices  78.8 us (35%)
  blocking collectives  77.1 us (34%)
  matrix products  27.5 us (12%)
  between operations  16.4 us (7%)
  other arithmetic  12.6 us (6%)
  local copies, waits for them, and re-layouts  6.69 us (3%)
  starting transfers between devices  6.69 us (3%)
    psum x1, waiting for transfers between devices, per_device(): branch_full = lax.psum(branch_part, 'state')  27.6 us
    psum x1, waiting for transfers between devices, per_device(): readout = lax.psum(read_part, 'state')  27.5 us
    unnamed x1, blocking collectives  19 us
    psum x1, blocking collectives, per_device(): projected = lax.psum(proj_part, 'head')  19 us
    unnamed x4, waiting for transfers between devices  18.2 us
    all_gather x1, blocking collectives, per_device(): lax.all_gather(normed, 'head', axis=0, tiled=True)  13.4 us
    psum x1, blocking collectives, per_device(): load_sum, prob_sum = lax.psum((load_own, prob_own), 'head')  12.1 us
    psum x1, blocking collectives, per_device(): first_sq = lax.psum(jnp.sum(tok_f32 * tok_f32, axis=1), 'state')  8.36 us
  transfers between devices with their start and end apart: 5, of which 4 were waited for; matrix products, arithmetic and copies ran while one was open for 3% of the time, Pallas kernels for 0%

commit v1 on v0

--- a/solution.py
+++ b/solution.py
@@ -56,7 +56,11 @@
         input_proj,
         preferred_element_type=jnp.float32,
     )
-    branch_full = lax.psum(branch_part, "state")
+    branch_full = branch_part
+    for hop in (1, 2):
+        branch_full = branch_full + lax.ppermute(
+            branch_full, "state", [(dev, dev ^ hop) for dev in range(4)]
+        )
     conv_input = branch_full[0]
     gate_branch = branch_full[1]
     window = jnp.concatenate([conv_state, conv_input[None]], axis=0)

time: 227 us -> 201 us (0.89)
  waiting for transfers between devices: 78.8 us -> 56 us
  matrix products: 27.5 us -> 25.1 us
    psum x1 -> x0, waiting for transfers between devices: 27.6 us -> none  [per_device(): branch_full = lax.psum(branch_part, 'state')]
    ppermute x0 -> x2, waiting for transfers between devices: none -> 4.78 us  [per_device(): lax.ppermute(branch_full, 'state', [(dev, dev ^ hop) for dev in range(4)])]
    unnamed x4 -> x3, waiting for transfers between devices: 18.2 us -> 18.2 us
  transfers between devices with their start and end apart: 5 -> 6, of which waited for: 4 -> 5; matrix products, arithmetic and copies ran while one was open for 3% -> 3% of each run, Pallas kernels for 0% -> 0%
where the time goes in v1:
time: 201 us; the launch traced here: 200 us
  blocking collectives  77.1 us (38%)
  waiting for transfers between devices  56 us (28%)
  matrix products  25.1 us (12%)
  between operations  16.7 us (8%)
  other arithmetic  12 us (6%)
  starting transfers between devices  7.2 us (4%)
  local copies, waits for them, and re-layouts  5.8 us (3%)
    psum x1, waiting for transfers between devices, per_device(): readout = lax.psum(read_part, 'state')  27.5 us
    psum x1, blocking collectives, per_device(): projected = lax.psum(proj_part, 'head')  19 us
    unnamed x1, blocking collectives  19 us
    unnamed x3, waiting for transfers between devices  18.2 us
    all_gather x1, blocking collectives, per_device(): lax.all_gather(normed, 'head', axis=0, tiled=True)  13.4 us
    psum x1, blocking collectives, per_device(): load_sum, prob_sum = lax.psum((load_own, prob_own), 'head')  12.1 us
    psum x1, blocking collectives, per_device(): first_sq = lax.psum(jnp.sum(tok_f32 * tok_f32, axis=1), 'state')  8.36 us
    dot_general x1, matrix products, expert_ffn(): jnp.einsum('nlcd,ldf->nlcf', received, up_proj, preferred_element_type=jn...  7.47 us
  transfers between devices with their start and end apart: 6, of which 5 were waited for; matrix products, arithmetic and copies ran while one was open for 3% of the time, Pallas kernels for 0%

profile of v1, /device:TPU:0, one launch (start us, length us, event | category | flops | bytes accessed | tf_op | source)
XLA Modules:
  0.0 200.0 jit_solution(13717176801125133689)
XLA Ops:
  7.3 0.9 fusion.46
  8.2 8.4 %psum.35 = f32[4]{0:T(128)S(1)} all-reduce(f32[4]{0:T(128)S(1)} %fusion.46), channel_id=1, replica_groups=mesh['groups'=2,'head'=4,'state'=4] {'state'}, use_global_device_ids=true, to_apply=%region_1.0 | all-reduce | flops 4 | bytes 32 | tf_op jit(solution)/shard_map/psum | solution.py:50
  16.6 0.8 fusion.52
  17.4 13.4 %all-gather = bf16[4,4,512]{2,1,0:T(4,128)(2,1)S(1)} all-gather(bf16[1,4,512]{2,1,0:T(4,128)(2,1)S(1)} %fusion.52), channel_id=1, replica_groups=mesh['groups'=2,'head'=4,'state'=4] {'head'}, dimensions={0}, use_global_device_ids=true | all-gather | bytes 20480 | tf_op jit(solution)/shard_map/all_gather | solution.py:55
  30.8 2.8 %convolution_bitcast_fusion = f32[2,16,2048]{2,1,0:T(8,128)S(1)} fusion(bf16[16,512,1]{1,0,2:T(8,128)(2,1)S(1)} %reshape.86, bf16[2,512,2048]{2,1,0:T(8,128)(2,1)} %param.23), kind=kOutput, calls=%fused_computation.6 | convolution fusion | flops 67108864 | bytes 4472832 | tf_op jit(solution)/shard_map/td,kdc->ktc/dot_general | solution.py:53
  33.7 0.8 iota_compare_fusion
  35.9 0.8 exp.33
  36.7 1.2 dynamic-slice
  39.3 4.7 %collective-permute-done.1 = f32[2,16,2048]{2,1,0:T(8,128)S(1)} collective-permute-done((f32[2,16,2048]{2,1,0:T(8,128)S(1)}, f32[2,16,2048]{2,1,0:T(8,128)S(1)}, u32[]{:S(2)}, u32[]{:S(2)}) %collective-permute-start.1) | collective-permute-done | bytes 262176 | tf_op jit(solution)/shard_map/ppermute | solution.py:61
  44.0 1.1 fusion.26
  45.1 0.7 divide_multiply_fusion
  45.8 1.7 fusion.31
  47.5 19.0 %psum.36 = f32[16,288]{1,0:T(8,128)S(1)} all-reduce(f32[16,288]{1,0:T(8,128)S(1)} %fusion.31), channel_id=1, replica_groups=mesh['groups'=2,'head'=4,'state'=4] {'head'}, use_global_device_ids=true, to_apply=%region_3.4 | all-reduce | flops 4608 | bytes 36864 | tf_op jit(solution)/shard_map/psum | solution.py:72
  66.9 1.5 fusion.56
  68.4 2.7 %multiply_reduce_fusion = (f32[16,2048]{1,0:T(8,128)}, f32[4,16,2048]{2,1,0:T(8,128)}) fusion(f32[4,16]{1,0:T(4,128)S(1)} %copy.53, f32[16,2048]{1,0:T(8,128)S(1)} %divide_multiply_fusion, f32[4,16]{1,0:T(4,128)S(1)} %copy.54, f32[16,2048]{1,0:T(8,128)S(1)} %get-tuple-element.14, f32[4,16,2048]{2,1,0:T(8,128)} %param.33, f32[4,2048]{1,0:T(4,128)S(1)} %exp.33, ...), kind=kLoop, calls=%fused_computation.23 | loop fusion | flops 884736 | bytes 1606144 | tf_op jit(solution)/shard_map/reduce_sum | solution.py:86
  71.2 1.7 fusion.27
  72.9 27.5 %all-reduce.4.cloned.1.call-done = f32[16,2048]{1,0:T(8,128)} async-done(((f32[16,2048]{1,0:T(8,128)}), f32[16,2048]{1,0:T(8,128)}) %all-reduce.4.cloned.1.call-update) | async-done | bytes 131088 | tf_op jit(solution)/shard_map/psum | solution.py:87
  100.4 1.3 fusion.28
  101.7 19.0 %all-reduce = f32[16,512]{1,0:T(8,128)S(1)} all-reduce(f32[16,512]{1,0:T(8,128)S(1)} %fusion.28), channel_id=2, replica_groups=mesh['groups'=2,'head'=4,'state'=4] {'head'}, use_global_device_ids=true, to_apply=%region_7.8.clone | all-reduce | flops 8192 | bytes 65536
  120.7 5.2 %all_gather.7 = bf16[4,2048]{1,0:T(4,128)(2,1)S(1)} all-gather(bf16[4,512]{1,0:T(4,128)(2,1)S(1)} %fusion.49), channel_id=1, replica_groups=mesh['groups'=2,'head'=4,'state'=4] {'state'}, dimensions={1}, use_global_device_ids=true | all-gather | bytes 20480 | tf_op jit(solution)/shard_map/all_gather | solution.py:96
  126.5 0.7 copy.63
  127.2 3.3 %all-to-all-start = ((bf16[4,2,2,2048]{3,2,1,0:T(2,128)(2,1)}), bf16[4,2,2,2048]{3,2,1,0:T(2,128)(2,1)S(1)}, u32[]{:S(2)}, u32[]{:S(2)}) async-start(bf16[4,2,2,2048]{3,2,1,0:T(2,128)(2,1)} %bitcast.6), calls=%async_computation | async-start | bytes 131072 | tf_op jit(solution)/shard_map/all_to_all | solution.py:123
  130.7 12.1 %all-reduce.1 = (f32[8]{0:T(128)S(1)}, f32[8]{0:T(128)S(1)}) all-reduce(f32[8]{0:T(128)S(1)} %get-tuple-element.5, f32[8]{0:T(128)S(1)} %get-tuple-element.15), channel_id=1, replica_groups=mesh['groups'=2,'head'=4,'state'=4] {'head'}, use_global_device_ids=true, to_apply=%region_14.15 | all-reduce | flops 16 | bytes 128 | tf_op jit(solution)/shard_map/psum | solution.py:144
  142.9 7.5 %fusion.6 = f32[4,2,2,1792]{3,0,2,1:T(4,128)S(1)} fusion(bf16[2,2048,1792]{2,1,0:T(8,128)(2,1)} %param.39, bf16[4,2,2,2048]{3,2,1,0:T(2,128)(2,1)S(1)} %all-to-all-done), kind=kOutput, calls=%fused_computation.7 | convolution fusion | flops 117440512 | bytes 14860288 | tf_op jit(solution)/shard_map/nlcd,ldf->nlcf/dot_general | solution.py:17
  150.4 7.5 %fusion.15 = bf16[4,2,2,1792]{3,0,2,1:T(4,128)(2,1)S(1)} fusion(bf16[2,2048,1792]{2,1,0:T(8,128)(2,1)} %param.40, f32[4,2,2,1792]{3,0,2,1:T(4,128)S(1)} %fusion.6, bf16[4,2,2,2048]{3,2,1,0:T(2,128)(2,1)S(1)} %all-to-all-done), kind=kOutput, calls=%fused_computation.11 | convolution fusion | flops 117612544 | bytes 14917632 | tf_op jit(solution)/shard_map/nlcd,ldf->nlcf/dot_general | solution.py:18
  157.9 2.1 %fusion.21 = bf16[4,2,2,2048]{3,0,2,1:T(4,128)(2,1)S(1)} fusion(bf16[4,2,2,1792]{3,0,2,1:T(4,128)(2,1)S(1)} %fusion.15, bf16[2,1792,2048]{2,1,0:T(8,128)(2,1)S(1)} %bitcast.72), kind=kOutput, calls=%fused_computation.14 | convolution fusion | flops 117473280 | bytes 14802944 | tf_op jit(solution)/shard_map/nlcf,lfd->nlcd/dot_general | solution.py:20
  160.0 0.7 copy.58
  160.7 3.3 %all-to-all-start.1 = ((bf16[4,2,2,2048]{3,2,1,0:T(2,128)(2,1)}), bf16[4,2,2,2048]{3,2,1,0:T(2,128)(2,1)S(1)}, u32[]{:S(2)}, u32[]{:S(2)}) async-start(bf16[4,2,2,2048]{3,2,1,0:T(2,128)(2,1)} %copy.58), calls=%async_computation.1 | async-start | bytes 131072 | tf_op jit(solution)/shard_map/all_to_all | solution.py:128
  164.1 5.6 %all-to-all-done.1 = bf16[4,2,2,2048]{3,2,1,0:T(2,128)(2,1)S(1)} async-done(((bf16[4,2,2,2048]{3,2,1,0:T(2,128)(2,1)}), bf16[4,2,2,2048]{3,2,1,0:T(2,128)(2,1)S(1)}, u32[]{:S(2)}, u32[]{:S(2)}) %all-to-all-start.1) | async-done | bytes 65568 | tf_op jit(solution)/shard_map/all_to_all | solution.py:128
  170.0 1.1 copy.64
  172.3 18.1 %reduce-scatter.4.cloned.1.call-done = bf16[512,4]{1,0:T(8,128)(2,1)} async-done(((bf16[2048,4]{1,0:T(8,128)(2,1)}), bf16[512,4]{1,0:T(8,128)(2,1)}) %reduce-scatter.4.cloned.1.call-update) | async-done | bytes 4112
  190.4 1.0 copy.65
  (56 shorter events, 5.1 us)
Async XLA Ops:
  7.2 93.2 %copy-start = (bf16[2048,512]{1,0:T(8,128)(2,1)S(1)}, bf16[2048,512]{1,0:T(8,128)(2,1)}, u32[]{:S(2)}) copy-start(bf16[2048,512]{1,0:T(8,128)(2,1)} %param.34) | copy-start | bytes 6291460
  7.2 113.5 %copy-start.1 = (bf16[4,512]{1,0:T(4,128)(2,1)S(1)}, bf16[4,512]{1,0:T(4,128)(2,1)}, u32[]{:S(2)}) copy-start(bf16[4,512]{1,0:T(4,128)(2,1)} %param.21) | copy-start | bytes 12292
  7.2 123.3 %copy-start.3 = (s32[4,2]{0,1:T(2,128)S(1)}, s32[4,2]{0,1:T(2,128)}, u32[]{:S(2)}) copy-start(s32[4,2]{0,1:T(2,128)} %param.37) | copy-start | bytes 100
  7.2 123.5 %copy-start.4 = (s32[4,2]{0,1:T(2,128)S(1)}, s32[4,2]{0,1:T(2,128)}, u32[]{:S(2)}) copy-start(s32[4,2]{0,1:T(2,128)} %param.38) | copy-start | bytes 100
  7.2 118.8 %copy-start.2 = (f32[2048]{0:T(1024)S(1)}, f32[2048]{0:T(1024)}, u32[]{:S(2)}) copy-start(f32[2048]{0:T(1024)} %param.35) | copy-start | bytes 24580
  7.2 118.8 %copy-start.5 = (f32[2048,8]{0,1:T(8,128)S(1)}, f32[2048,8]{0,1:T(8,128)}, u32[]{:S(2)}) copy-start(f32[2048,8]{0,1:T(8,128)} %param.36) | copy-start | bytes 196612
  7.2 93.1 %all-reduce.4.cloned.1.call-start = ((), (), s32[]{:S(2)}) async-start(), calls=%async_computation.3 | async-start | bytes 262144 | tf_op jit(solution)/shard_map/psum | solution.py:87
  33.7 1.5 collective-permute-start
  35.3 8.7 %collective-permute-start.1 = (f32[2,16,2048]{2,1,0:T(8,128)S(1)}, f32[2,16,2048]{2,1,0:T(8,128)S(1)}, u32[]{:S(2)}, u32[]{:S(2)}) collective-permute-start(f32[2,16,2048]{2,1,0:T(8,128)S(1)} %add.107), channel_id=1, source_target_pairs={{0,2},{1,3},{2,0},{3,1},{4,6},{5,7},{6,4},{7,5},{8,10},{9,11},{10,... | collective-permute-start | bytes 786440 | tf_op jit(solution)/shard_map/ppermute | solution.py:61
  127.2 15.7 %all-to-all-start = ((bf16[4,2,2,2048]{3,2,1,0:T(2,128)(2,1)}), bf16[4,2,2,2048]{3,2,1,0:T(2,128)(2,1)S(1)}, u32[]{:S(2)}, u32[]{:S(2)}) async-start(bf16[4,2,2,2048]{3,2,1,0:T(2,128)(2,1)} %bitcast.6), calls=%async_computation | async-start | bytes 131072 | tf_op jit(solution)/shard_map/all_to_all | solution.py:123
  142.9 28.1 %copy-start.6 = (f32[8]{0:T(128)}, f32[8]{0:T(128)S(1)}, u32[]{:S(2)}) copy-start(f32[8]{0:T(128)S(1)} %get-tuple-element.7) | copy-start | bytes 100
  142.9 15.0 %slice-start = ((s8[14680064]{0:T(1024)(128)(4,1)}), s8[4194304]{0:T(1024)(128)(4,1)S(1)}, s32[]{:S(2)}) async-start(s8[14680064]{0:T(1024)(128)(4,1)} %bitcast.71), calls=%async_computation.5 | async-start | bytes 8388608
  142.9 15.0 %slice-start.1 = ((s8[14680064]{0:T(1024)(128)(4,1)}), s8[4194304]{0:T(1024)(128)(4,1)S(1)}, s32[]{:S(2)}) async-start(s8[14680064]{0:T(1024)(128)(4,1)} %bitcast.71), calls=%async_computation.6 | async-start | bytes 8388608
  150.4 7.5 %slice-start.2 = ((s8[14680064]{0:T(1024)(128)(4,1)}), s8[4194304]{0:T(1024)(128)(4,1)S(1)}, s32[]{:S(2)}) async-start(s8[14680064]{0:T(1024)(128)(4,1)} %bitcast.71), calls=%async_computation.7 | async-start | bytes 8388608
  150.4 7.5 %slice-start.3 = ((s8[14680064]{0:T(1024)(128)(4,1)}), s8[2097152]{0:T(1024)(128)(4,1)S(1)}, s32[]{:S(2)}) async-start(s8[14680064]{0:T(1024)(128)(4,1)} %bitcast.71), calls=%async_computation.8 | async-start | bytes 4194304
  160.7 9.0 %all-to-all-start.1 = ((bf16[4,2,2,2048]{3,2,1,0:T(2,128)(2,1)}), bf16[4,2,2,2048]{3,2,1,0:T(2,128)(2,1)S(1)}, u32[]{:S(2)}, u32[]{:S(2)}) async-start(bf16[4,2,2,2048]{3,2,1,0:T(2,128)(2,1)} %copy.58), calls=%async_computation.1 | async-start | bytes 131072 | tf_op jit(solution)/shard_map/all_to_all | solution.py:128
  164.0 26.4 %reduce-scatter.4.cloned.1.call-start = ((), (), s32[]{:S(2)}) async-start(), calls=%async_computation.4 | async-start | bytes 655360
Sparse Core Ops, SparseCore 0:
  71.3 29.0 all-reduce.3
  171.1 19.2 reduce-scatter.3
